TPU v7x, 128 devices: a whole 4x4x4 slice. The times are simulated.
128 devices in a mesh: part: 1, tp: 2 (over core), dp: 64 (over z, y, x).
Axes of the slice: x: 4, y: 4, z: 4, core: 2. Of those that a mesh axis runs over, the one named last changes fastest.
Arguments:
- hidden: bfloat16 [128, 2048, 768], P(('part', 'dp', 'tp'))
- ln_gain: float32 [768], replicated
- w_in: bfloat16 [768, 7040], P(None, ('dp', 'tp'))
- w_out: bfloat16 [3840, 768], P(('dp', 'tp'))
Outputs:
- output 1: bfloat16 [128, 2048, 768], P(('part', 'dp', 'tp'))
- output 2: bfloat16 [128, 2048, 64], P(('part', 'dp', 'tp'))
- output 3: bfloat16 [128, 2048, 64], P(('part', 'dp', 'tp'))
All inputs are finite; a program needn't handle non-finite values.
Results may differ from a plain program's by a relative error of at most 0.00275064.
Values are sent between devices in bfloat16 or wider.
A program may use at most 1 GiB of HBM per device.

v0:
```python
import jax
import jax.numpy as jnp
from jax import lax
from jax.sharding import PartitionSpec as P

LN_EPS = 1e-6
ROPE_BASE = 10000.0
BLOCK_CAP = 512


def layer_norm(x_blk, ln_gain):
    x_wide = x_blk.astype(jnp.float32)
    centered = x_wide - jnp.mean(x_wide, axis=-1, keepdims=True)
    row_var = jnp.mean(centered * centered, axis=-1, keepdims=True)
    return (centered * lax.rsqrt(row_var + LN_EPS) * ln_gain).astype(jnp.bfloat16)


def rotary(values):
    seq_len = values.shape[1]
    head_dim = values.shape[-1]
    half_dim = head_dim // 2
    inv_freq = ROPE_BASE ** (-jnp.arange(half_dim, dtype=jnp.float32) * 2.0 / head_dim)
    angles = jnp.arange(seq_len, dtype=jnp.float32)[:, None] * inv_freq[None, :]
    tab_shape = (1, seq_len) + (1,) * (values.ndim - 3) + (half_dim,)
    cos_tab = jnp.cos(angles).reshape(tab_shape)
    sin_tab = jnp.sin(angles).reshape(tab_shape)
    first_half = values[..., :half_dim]
    second_half = values[..., half_dim:]
    return jnp.concatenate([first_half * cos_tab - second_half * sin_tab,
                            second_half * cos_tab + first_half * sin_tab], axis=-1)


def causal_mqa(q_rot, k_rot, v_all):
    n_batch, seq_len, n_heads, head_dim = q_rot.shape
    q_blk = min(seq_len, BLOCK_CAP)
    n_blk = seq_len // q_blk
    q_tiles = q_rot.reshape(n_batch, n_blk, q_blk, n_heads, head_dim)
    score_scale = head_dim ** -0.5
    key_pos = jnp.arange(seq_len)

    def one_block(blk_idx):
        q_tile = lax.dynamic_index_in_dim(q_tiles, blk_idx, axis=1, keepdims=False)
        scores = jnp.einsum('bqhe,bke->bqhk', q_tile, k_rot, preferred_element_type=jnp.float32) * score_scale
        q_pos = blk_idx * q_blk + jnp.arange(q_blk)
        allowed = key_pos[None, :] <= q_pos[:, None]
        scores = jnp.where(allowed[None, :, None, :], scores, -1e30)
        attn_prob = jax.nn.softmax(scores, axis=-1).astype(jnp.bfloat16)
        return jnp.einsum('bqhk,bke->bqhe', attn_prob, v_all, preferred_element_type=jnp.float32).astype(jnp.bfloat16)

    out_tiles = lax.map(one_block, jnp.arange(n_blk))
    return jnp.moveaxis(out_tiles, 0, 1).reshape(n_batch, seq_len, n_heads * head_dim)


def mix_rows(joint_rows, q_width, head_dim):
    n_batch, seq_len, joint_width = joint_rows.shape
    ff_width = (joint_width - q_width - 2 * head_dim) // 2
    gate_at = q_width + 2 * head_dim
    q_raw = joint_rows[..., :q_width].reshape(n_batch, seq_len, q_width // head_dim, head_dim)
    k_raw = joint_rows[..., q_width:q_width + head_dim]
    v_all = joint_rows[..., q_width + head_dim:gate_at]
    gate_proj = joint_rows[..., gate_at:gate_at + ff_width]
    up_proj = joint_rows[..., gate_at + ff_width:]
    q_rot = rotary(q_raw.astype(jnp.float32)).astype(jnp.bfloat16)
    k_rot = rotary(k_raw.astype(jnp.float32)).astype(jnp.bfloat16)
    attn_out = causal_mqa(q_rot, k_rot, v_all)
    mlp_out = (jax.nn.silu(gate_proj.astype(jnp.float32)) * up_proj.astype(jnp.float32)).astype(jnp.bfloat16)
    return jnp.concatenate([attn_out, mlp_out], axis=-1), k_rot, v_all


def solution(mesh):
    tok_spec = P(('part', 'dp', 'tp'))

    def per_device(x_blk, ln_gain, w_in_blk, w_out_blk):
        w_in = lax.all_gather(w_in_blk, ('dp', 'tp'), axis=1, tiled=True)
        w_out = lax.all_gather(w_out_blk, ('dp', 'tp'), axis=0, tiled=True)
        ff_width = 4 * x_blk.shape[-1]
        q_width = w_out.shape[0] - ff_width
        head_dim = (w_in.shape[1] - w_out.shape[0] - ff_width) // 2
        h_rows = layer_norm(x_blk, ln_gain)
        joint_rows = jnp.einsum('bsd,dc->bsc', h_rows, w_in, preferred_element_type=jnp.float32).astype(jnp.bfloat16)
        mixed_rows, k_rot, v_all = mix_rows(joint_rows, q_width, head_dim)
        proj_out = jnp.einsum('bsz,zd->bsd', mixed_rows, w_out, preferred_element_type=jnp.float32)
        y_blk = (x_blk.astype(jnp.float32) + proj_out).astype(jnp.bfloat16)
        return y_blk, k_rot, v_all

    return jax.shard_map(per_device, mesh=mesh,
                         in_specs=(tok_spec, P(), P(None, ('dp', 'tp')), P(('dp', 'tp'), None)),
                         out_specs=(tok_spec, tok_spec, tok_spec), check_vma=False)
```

profile of v0, /device:TPU:1, one launch (start us, length us, event | category | flops | bytes accessed | tf_op | source)
XLA Modules:
  0.0 461.4 jit_solution(10528901188141576134)
XLA Ops:
  7.2 0.0 all-gather.7.cloned.1.call-start
  7.2 0.7 all-gather.7.cloned.1.call-update
  7.9 0.0 all-gather.5.cloned.1.call-start
  7.9 0.7 all-gather.5.cloned.1.call-update
  8.7 2.4 convert_reduce_fusion
  11.1 2.9 fusion.45
  14.0 1.8 fusion.57
  15.8 67.2 %all-gather.7.cloned.1.call-done = bf16[128,30,768]{2,1,0:T(8,128)(2,1)} async-done(((bf16[1,30,768]{2,1,0:T(8,128)(2,1)}), bf16[128,30,768]{2,1,0:T(8,128)(2,1)}) %all-gather.7.cloned.1.call-update) | async-done | bytes 5898256 | tf_op jit(solution)/shard_map/all_gather | solution.py:75
  83.0 9.4 %reshape.308 = bf16[3840,768]{1,0:T(8,128)(2,1)} reshape(bf16[128,30,768]{2,1,0:T(8,128)(2,1)} %all-gather.7.cloned.1.call-done) | data formatting | bytes 11796480
  92.4 62.4 %all-gather.5.cloned.1.call-done = bf16[128,55,768]{2,1,0:T(8,128)(2,1)} async-done(((bf16[1,55,768]{2,1,0:T(8,128)(2,1)}), bf16[128,55,768]{2,1,0:T(8,128)(2,1)}) %all-gather.5.cloned.1.call-update) | async-done | bytes 10813456 | tf_op jit(solution)/shard_map/all_gather | solution.py:74
  154.8 14.3 %reshape.306 = bf16[7040,768]{1,0:T(8,128)(2,1)} reshape(bf16[128,55,768]{2,1,0:T(8,128)(2,1)} %all-gather.5.cloned.1.call-done) | data formatting | bytes 21626880
  169.1 0.0 copy-done
  169.1 0.0 copy-done.6
  169.1 31.5 %convert_bitcast_fusion = bf16[1,2048,7040]{1,2,0:T(8,128)(2,1)} fusion(bf16[7040,768]{1,0:T(8,128)(2,1)} %reshape.306, bf16[1,2048,768]{2,1,0:T(8,128)(2,1)S(1)} %copy-done, f32[768]{0:T(1024)S(1)} %copy-done.6, f32[2048]{0:T(1024)S(1)} %add_rsqrt_fusion, f32[2048]{0:T(1024)S(1)} %broadcast_multiply_fusion), kind=kOutput, calls=%fused_computation.30 | convolution fusion | flops 22168207360 | bytes 42814464 | tf_op jit(solution)/shard_map/bsd,dc->bsc/dot_general | solution.py:80
  200.6 1.8 fusion.68
  202.4 16.9 %fusion.39 = bf16[1,2048,3072]{1,2,0:T(8,128)(2,1)} fusion(bf16[1,2048,7040]{1,2,0:T(8,128)(2,1)} %convert_bitcast_fusion), kind=kLoop, calls=%fused_computation.35 | loop fusion | flops 50331648 | bytes 37748736 | tf_op jit(solution)/shard_map/convert_element_type | solution.py:66
  219.3 1.8 subtract_convert_fusion.1
  221.1 0.0 slice-done
  221.1 0.8 convert.19
  221.9 0.0 copy-done.2
  221.9 1.1 subtract_convert_fusion
  223.0 2.4 concatenate.32
  225.4 1.3 concatenate.33
  226.8 0.0 copy-start.4
  226.8 3.5 pad_maximum_fusion
  230.3 2.4 copy.29
  232.7 0.0 copy-done.3
  232.7 189.8 %while.11 = (s32[]{:T(128)}, bf16[4,1,512,12,64]{2,4,3,1,0:T(8,128)(2,1)}, s32[4]{0:T(128)S(1)}, bf16[1,4,512,12,64]{2,4,3,1,0:T(8,128)(2,1)}, bf16[1,2048,64]{1...) while((s32[]{:T(128)}, ...), condition=%wide.region_5.6_spmd.clone, body=%wide.region_2.5_spmd.clone.sunk | while | flops 3298167296 | bytes 104911032 | solution.py:50
  232.7 0.6 dynamic_slice.29
  235.9 0.7 iota_compare_fusion.2
  236.6 24.4 %fusion.79 = (f32[512,12]{0,1:T(8,128)S(1)}, f32[512,12,2048]{2,0,1:T(8,128)}) fusion(pred[512,2048]{1,0:T(8,128)(4,1)S(1)} %iota_compare_fusion.2, bf16[1,4,512,12,64]{2,4,3,1,0:T(8,128)(2,1)} %get-tuple-element.174, s32[]{:T(128)S(6)} %select_n.24, bf16[1,2048,64]{1,2,0:T(8,128)(2,1)S(1)} %get-tuple-element.175), kind=kOutput, calls=%fused_computation.70.clone.1 | convolution fusion | flops 1660946432 | bytes 52453380 | tf_op jit(solution)/shard_map/while/body/eval_jaxpr/sub | solution.py:47
  261.0 19.2 %fusion.80 = bf16[4,1,512,12,64]{2,4,3,1,0:T(8,128)(2,1)} fusion(bf16[4,1,512,12,64]{2,4,3,1,0:T(8,128)(2,1)} %get-tuple-element.162, s32[]{:T(128)S(6)} %copy.35, f32[512,12,2048]{2,0,1:T(8,128)} %get-tuple-element.149, f32[512,12]{0,1:T(8,128)S(1)} %get-tuple-element.150, bf16[1,2048,64]{1,2,0:T(8,128)(2,1)S(1)} %get-tuple-element.176), kind=kOutput, calls=%fused_computation.14.clone.1 | convolution fusion | flops 1636171776 | bytes 51404804 | tf_op jit(solution)/shard_map/while/body/eval_jaxpr/bqhk,bke->bqhe/dot_general | solution.py:48
  280.2 0.6 dynamic_slice.29
  283.3 0.7 iota_compare_fusion.2
  284.0 24.4 %fusion.79 = (f32[512,12]{0,1:T(8,128)S(1)}, f32[512,12,2048]{2,0,1:T(8,128)}) fusion(pred[512,2048]{1,0:T(8,128)(4,1)S(1)} %iota_compare_fusion.2, bf16[1,4,512,12,64]{2,4,3,1,0:T(8,128)(2,1)} %get-tuple-element.174, s32[]{:T(128)S(6)} %select_n.24, bf16[1,2048,64]{1,2,0:T(8,128)(2,1)S(1)} %get-tuple-element.175), kind=kOutput, calls=%fused_computation.70.clone.1 | convolution fusion | flops 1660946432 | bytes 52453380 | tf_op jit(solution)/shard_map/while/body/eval_jaxpr/sub | solution.py:47
  308.4 19.2 %fusion.80 = bf16[4,1,512,12,64]{2,4,3,1,0:T(8,128)(2,1)} fusion(bf16[4,1,512,12,64]{2,4,3,1,0:T(8,128)(2,1)} %get-tuple-element.162, s32[]{:T(128)S(6)} %copy.35, f32[512,12,2048]{2,0,1:T(8,128)} %get-tuple-element.149, f32[512,12]{0,1:T(8,128)S(1)} %get-tuple-element.150, bf16[1,2048,64]{1,2,0:T(8,128)(2,1)S(1)} %get-tuple-element.176), kind=kOutput, calls=%fused_computation.14.clone.1 | convolution fusion | flops 1636171776 | bytes 51404804 | tf_op jit(solution)/shard_map/while/body/eval_jaxpr/bqhk,bke->bqhe/dot_general | solution.py:48
  327.6 0.6 dynamic_slice.29
  330.8 0.7 iota_compare_fusion.2
  331.4 24.4 %fusion.79 = (f32[512,12]{0,1:T(8,128)S(1)}, f32[512,12,2048]{2,0,1:T(8,128)}) fusion(pred[512,2048]{1,0:T(8,128)(4,1)S(1)} %iota_compare_fusion.2, bf16[1,4,512,12,64]{2,4,3,1,0:T(8,128)(2,1)} %get-tuple-element.174, s32[]{:T(128)S(6)} %select_n.24, bf16[1,2048,64]{1,2,0:T(8,128)(2,1)S(1)} %get-tuple-element.175), kind=kOutput, calls=%fused_computation.70.clone.1 | convolution fusion | flops 1660946432 | bytes 52453380 | tf_op jit(solution)/shard_map/while/body/eval_jaxpr/sub | solution.py:47
  355.8 19.2 %fusion.80 = bf16[4,1,512,12,64]{2,4,3,1,0:T(8,128)(2,1)} fusion(bf16[4,1,512,12,64]{2,4,3,1,0:T(8,128)(2,1)} %get-tuple-element.162, s32[]{:T(128)S(6)} %copy.35, f32[512,12,2048]{2,0,1:T(8,128)} %get-tuple-element.149, f32[512,12]{0,1:T(8,128)S(1)} %get-tuple-element.150, bf16[1,2048,64]{1,2,0:T(8,128)(2,1)S(1)} %get-tuple-element.176), kind=kOutput, calls=%fused_computation.14.clone.1 | convolution fusion | flops 1636171776 | bytes 51404804 | tf_op jit(solution)/shard_map/while/body/eval_jaxpr/bqhk,bke->bqhe/dot_general | solution.py:48
  375.0 0.6 dynamic_slice.29
  378.2 0.7 iota_compare_fusion.2
  378.9 24.4 %fusion.79 = (f32[512,12]{0,1:T(8,128)S(1)}, f32[512,12,2048]{2,0,1:T(8,128)}) fusion(pred[512,2048]{1,0:T(8,128)(4,1)S(1)} %iota_compare_fusion.2, bf16[1,4,512,12,64]{2,4,3,1,0:T(8,128)(2,1)} %get-tuple-element.174, s32[]{:T(128)S(6)} %select_n.24, bf16[1,2048,64]{1,2,0:T(8,128)(2,1)S(1)} %get-tuple-element.175), kind=kOutput, calls=%fused_computation.70.clone.1 | convolution fusion | flops 1660946432 | bytes 52453380 | tf_op jit(solution)/shard_map/while/body/eval_jaxpr/sub | solution.py:47
  403.3 19.2 %fusion.80 = bf16[4,1,512,12,64]{2,4,3,1,0:T(8,128)(2,1)} fusion(bf16[4,1,512,12,64]{2,4,3,1,0:T(8,128)(2,1)} %get-tuple-element.162, s32[]{:T(128)S(6)} %copy.35, f32[512,12,2048]{2,0,1:T(8,128)} %get-tuple-element.149, f32[512,12]{0,1:T(8,128)S(1)} %get-tuple-element.150, bf16[1,2048,64]{1,2,0:T(8,128)(2,1)S(1)} %get-tuple-element.176), kind=kOutput, calls=%fused_computation.14.clone.1 | convolution fusion | flops 1636171776 | bytes 51404804 | tf_op jit(solution)/shard_map/while/body/eval_jaxpr/bqhk,bke->bqhe/dot_general | solution.py:48
  422.5 0.7 copy-done.5
  423.2 6.2 %copy.30 = bf16[4,1,512,12,64]{2,0,4,3,1:T(4,128)(2,1)} copy(bf16[4,1,512,12,64]{2,4,3,1,0:T(8,128)(2,1)} %get-tuple-element.40) | data formatting | bytes 6291456 | tf_op jit(solution)/shard_map/while | solution.py:50
  429.3 6.1 %reshape_transpose.3 = bf16[1,2048,768]{1,2,0:T(8,128)(2,1)} reshape(bf16[4,1,512,12,64]{2,0,4,3,1:T(4,128)(2,1)} %copy.30) | data formatting | bytes 6291456 | tf_op jit(solution)/shard_map/reshape;transpose | solution.py:51
  435.4 19.1 %fusion.48 = bf16[1,2048,768]{2,1,0:T(8,128)(2,1)} fusion(bf16[1,2048,768]{2,1,0:T(8,128)(2,1)S(1)} %copy-done.1, bf16[3840,768]{1,0:T(8,128)(2,1)} %reshape.308, bf16[1,2048,3072]{1,2,0:T(8,128)(2,1)} %fusion.39, bf16[1,2048,768]{1,2,0:T(8,128)(2,1)} %reshape_transpose.3), kind=kOutput, calls=%fused_computation.48 | convolution fusion | flops 12115771392 | bytes 27918336 | tf_op jit(solution)/shard_map/bsz,zd->bsd/dot_general | solution.py:82
  (19 shorter events, 0.1 us)
Async XLA Ops:
  7.2 75.8 %all-gather.7.cloned.1.call-start = ((), (), s32[]{:S(2)}) async-start(), calls=%async_computation.1 | async-start | bytes 6340608 | tf_op jit(solution)/shard_map/all_gather | solution.py:75
  7.9 146.9 %all-gather.5.cloned.1.call-start = ((), (), s32[]{:S(2)}) async-start(), calls=%async_computation | async-start | bytes 11096064 | tf_op jit(solution)/shard_map/all_gather | solution.py:74
  92.4 76.7 %copy-start = (bf16[1,2048,768]{2,1,0:T(8,128)(2,1)S(1)}, bf16[1,2048,768]{2,1,0:T(8,128)(2,1)}, u32[]{:S(2)}) copy-start(bf16[1,2048,768]{2,1,0:T(8,128)(2,1)} %param.6) | copy-start | bytes 9437188
  92.4 76.7 %copy-start.6 = (f32[768]{0:T(1024)S(1)}, f32[768]{0:T(1024)}, u32[]{:S(2)}) copy-start(f32[768]{0:T(1024)} %param.7) | copy-start | bytes 9220
  202.4 18.7 %slice-start = ((bf16[1,2048,7040]{1,2,0:T(8,128)(2,1)}), bf16[1,2048,768]{1,2,0:T(8,128)(2,1)S(1)}, s32[]{:S(2)}) async-start(bf16[1,2048,7040]{1,2,0:T(8,128)(2,1)} %convert_bitcast_fusion), calls=%async_computation.2 | async-start | bytes 6291456 | tf_op jit(solution)/shard_map/slice | solution.py:58
  219.3 2.6 copy-start.2
  226.8 5.9 %copy-start.3 = (bf16[1,2048,32]{1,2,0:T(8,128)(2,1)S(1)}, bf16[1,2048,32]{1,2,0:T(8,128)(2,1)}, u32[]{:S(2)}) copy-start(bf16[1,2048,32]{1,2,0:T(8,128)(2,1)} %get-tuple-element.107) | copy-start | bytes 393220
  226.8 5.9 %copy-start.4 = (bf16[1,2048,64]{1,2,0:T(8,128)(2,1)S(1)}, bf16[1,2048,64]{1,2,0:T(8,128)(2,1)}, u32[]{:S(2)}) copy-start(bf16[1,2048,64]{1,2,0:T(8,128)(2,1)} %get-tuple-element.156) | copy-start | bytes 786436
  422.5 0.7 copy-start.5
  423.2 12.3 %copy-start.1 = (bf16[1,2048,768]{2,1,0:T(8,128)(2,1)S(1)}, bf16[1,2048,768]{2,1,0:T(8,128)(2,1)}, u32[]{:S(2)}) copy-start(bf16[1,2048,768]{2,1,0:T(8,128)(2,1)} %param.6) | copy-start | bytes 9437188
Sparse Core Ops, SparseCore 0:
  11.1 71.8 all-gather.6
  86.0 68.7 all-gather.4
where the time goes:
time: 463 us; the launch traced here: 461 us
  matrix products  225 us (49%)
  waiting for transfers between devices  131 us (28%)
  local copies, waits for them, and re-layouts  45.2 us (10%)
  other arithmetic  35.6 us (8%)
  between operations  14.2 us (3%)
  loops' own time  10.4 us (2%)
    sub x4, matrix products, one_block(): attn_prob = jax.nn.softmax(scores, axis=-1).astype(jnp.bfloat16)  97.6 us
    dot_general x4, matrix products, one_block(): jnp.einsum('bqhk,bke->bqhe', attn_prob, v_all, preferred_element_type=jnp...  76.7 us
    all_gather x1, waiting for transfers between devices, per_device(): w_out = lax.all_gather(w_out_blk, ('dp', 'tp'), axis=0, tiled=True)  67.2 us
    all_gather x1, waiting for transfers between devices, per_device(): w_in = lax.all_gather(w_in_blk, ('dp', 'tp'), axis=1, tiled=True)  62.4 us
    dot_general x1, matrix products, per_device(): jnp.einsum('bsd,dc->bsc', h_rows, w_in, preferred_element_type=jnp.float32)  31.5 us
    unnamed x17, local copies, waits for them, and re-layouts  26.8 us
    dot_general x1, matrix products, per_device(): jnp.einsum('bsz,zd->bsd', mixed_rows, w_out, preferred_element_type=jnp.f...  19.1 us
    convert_element_type x1, other arithmetic, mix_rows(): (jax.nn.silu(gate_proj.astype(jnp.float32)) * up_proj.astype(jnp.float32)...  16.9 us
  transfers between devices with their start and end apart: 2, of which 2 were waited for; matrix products, arithmetic and copies ran while one was open for 4% of the time, Pallas kernels for 0%

commit v1 on v0

v1 whole, which is shorter than its diff:
```python
import functools

import jax
import jax.numpy as jnp
import numpy as np
from jax import lax
from jax.experimental import pallas as pl
from jax.experimental.pallas import tpu as pltpu
from jax.sharding import PartitionSpec as P

LN_EPS = 1e-6
ROPE_BASE = 10000.0
LOG2E = 1.4426950408889634
TILE = 256
FF_CHUNK = 512
ROW_CHUNK = 512
F32 = jnp.float32
BF16 = jnp.bfloat16


def dot_nt(a, b):
    return lax.dot_general(a, b, (((1,), (1,)), ((), ())), preferred_element_type=F32)


def rope_tables(seq_len, head_dim):
    half_dim = head_dim // 2
    inv_freq = ROPE_BASE ** (-np.arange(half_dim, dtype=np.float64) * 2.0 / head_dim)
    angles = inv_freq.astype(np.float32).astype(np.float64)[:, None] * np.arange(seq_len)[None, :]
    angles = angles.astype(np.float32).astype(np.float64)
    return np.cos(angles).astype(np.float32), np.sin(angles).astype(np.float32)


def attention_body(heads, head_dim, x_ref, gain_ref, wq_ref, cos_ref, sin_ref, h_ref, attn_ref, kt_ref, vt_ref,
                   qt, ks, s_a, s_b, ot):
    seq_len, width = x_ref.shape
    q_width = heads * head_dim
    half = head_dim // 2
    n_tiles = seq_len // TILE

    def norm_rows(t, carry):
        rows = pl.ds(pl.multiple_of(t * TILE, TILE), TILE)
        x_wide = x_ref[rows, :].astype(F32)
        centered = x_wide - jnp.mean(x_wide, axis=-1, keepdims=True)
        row_var = jnp.mean(centered * centered, axis=-1, keepdims=True)
        h_ref[rows, :] = (centered * lax.rsqrt(row_var + LN_EPS) * gain_ref[...]).astype(BF16)
        return carry

    lax.fori_loop(0, n_tiles, norm_rows, 0)

    def project(t, carry):
        cols = pl.ds(pl.multiple_of(t * TILE, TILE), TILE)
        pt = dot_nt(wq_ref[...], h_ref[cols, :]).astype(BF16)
        cos_t = cos_ref[:, cols]
        sin_t = sin_ref[:, cols]
        for g in range(heads + 1):
            a = pt[g * head_dim:g * head_dim + half, :].astype(F32)
            b = pt[g * head_dim + half:(g + 1) * head_dim, :].astype(F32)
            rot = jnp.concatenate([a * cos_t - b * sin_t, b * cos_t + a * sin_t], axis=0)
            if g < heads:
                qt[g * head_dim:(g + 1) * head_dim, cols] = rot.astype(BF16)
            else:
                kt_ref[:, cols] = rot.astype(BF16)
                ks[cols, :] = rot.T.astype(BF16)
        vt_ref[:, cols] = pt[q_width + head_dim:q_width + 2 * head_dim, :]
        return carry

    lax.fori_loop(0, n_tiles, project, 0)

    coef = LOG2E * head_dim ** -0.5

    for i in range(n_tiles):
        cols = slice(i * TILE, (i + 1) * TILE)

        def score_tile(h, j, s_ref, m8):
            rows = slice(j * TILE, (j + 1) * TILE)
            hd = pl.ds(pl.multiple_of(h * head_dim, head_dim), head_dim)
            s = jnp.dot(ks[rows, :], qt[hd, cols], preferred_element_type=F32)
            if j == i:
                key = lax.broadcasted_iota(jnp.int32, (TILE, TILE), 0)
                qry = lax.broadcasted_iota(jnp.int32, (TILE, TILE), 1)
                s = jnp.where(key <= qry, s, -1e30)
            s_ref[rows, :] = s
            top = jnp.max(s.reshape(TILE // 8, 8, TILE), axis=0)
            return top if m8 is None else jnp.maximum(m8, top)

        def mix_tile(j, s_ref, m, l8, acc):
            rows = slice(j * TILE, (j + 1) * TILE)
            p = jnp.exp2((s_ref[rows, :] - m) * coef)
            part = jnp.sum(p.reshape(TILE // 8, 8, TILE), axis=0)
            o = jnp.dot(vt_ref[:, rows], p.astype(BF16), preferred_element_type=F32)
            return (part, o) if l8 is None else (l8 + part, acc + o)

        def finish(h, l8, acc):
            hd = pl.ds(pl.multiple_of(h * head_dim, head_dim), head_dim)
            ot[hd, :] = (acc / jnp.sum(l8, axis=0, keepdims=True)).astype(BF16)

        def step(h_mix, s_mix, m_mix, h_next, s_next):
            m8 = l8 = acc = None
            m = jnp.max(m_mix, axis=0, keepdims=True)
            for j in range(i + 1):
                m8 = score_tile(h_next, j, s_next, m8)
                l8, acc = mix_tile(j, s_mix, m, l8, acc)
            finish(h_mix, l8, acc)
            return m8

        m8 = None
        for j in range(i + 1):
            m8 = score_tile(0, j, s_a, m8)

        def pair(t, m8):
            h = 2 * t
            m8_b = step(h, s_a, m8, h + 1, s_b)
            return step(h + 1, s_b, m8_b, jnp.minimum(h + 2, heads - 1), s_a)

        lax.fori_loop(0, heads // 2, pair, m8)
        attn_ref[cols, :] = ot[...].T


def attention_call(x, gain, wq, cos_t, sin_t, heads, head_dim):
    seq_len, width = x.shape
    q_width = heads * head_dim
    vmem = pl.BlockSpec(memory_space=pltpu.VMEM)
    return pl.pallas_call(
        functools.partial(attention_body, heads, head_dim),
        out_shape=(jax.ShapeDtypeStruct((seq_len, width), BF16),
                   jax.ShapeDtypeStruct((seq_len, q_width), BF16),
                   jax.ShapeDtypeStruct((head_dim, seq_len), BF16),
                   jax.ShapeDtypeStruct((head_dim, seq_len), BF16)),
        in_specs=[vmem] * 5,
        out_specs=(vmem,) * 4,
        scratch_shapes=[
            pltpu.VMEM((q_width, seq_len), BF16),
            pltpu.VMEM((seq_len, head_dim), BF16),
            pltpu.VMEM((seq_len, TILE), F32),
            pltpu.VMEM((seq_len, TILE), F32),
            pltpu.VMEM((q_width, TILE), BF16),
        ],
        compiler_params=pltpu.CompilerParams(vmem_limit_bytes=60 * 1024 * 1024),
        name="attention",
    )(x, gain, wq, cos_t, sin_t)


def mlp_body(h_ref, attn_ref, x_ref, wg_ref, wu_ref, wd_ref, wa_ref, y_ref, acc):
    j = pl.program_id(0)
    last = pl.num_programs(0) - 1
    n_rows = h_ref.shape[0] // ROW_CHUNK

    def rows_of(t):
        return pl.ds(t * ROW_CHUNK, ROW_CHUNK)

    @pl.when(j == 0)
    def _():
        for t in range(n_rows):
            r = rows_of(t)
            acc[r, :] = x_ref[r, :].astype(F32) + jnp.dot(attn_ref[r, :], wa_ref[...], preferred_element_type=F32)

    for t in range(n_rows):
        r = rows_of(t)
        gate = dot_nt(h_ref[r, :], wg_ref[...]).astype(BF16).astype(F32)
        up = dot_nt(h_ref[r, :], wu_ref[...]).astype(BF16).astype(F32)
        m = (gate * jax.nn.sigmoid(gate) * up).astype(BF16)
        acc[r, :] += jnp.dot(m, wd_ref[...], preferred_element_type=F32)

    @pl.when(j == last)
    def _():
        y_ref[...] = acc[...].astype(BF16)


def mlp_call(h, attn, x, w_in_t, w_out, gate_at, ff_width):
    seq_len, width = x.shape
    q_width = attn.shape[1]
    whole = pl.BlockSpec((seq_len, width), lambda j: (0, 0))
    n_chunks = ff_width // FF_CHUNK

    def rows_from(start):
        return pl.BlockSpec((pl.Element(FF_CHUNK), pl.Element(width)), lambda j: ((start // 16 + j * (FF_CHUNK // 16)) * 16, 0))

    return pl.pallas_call(
        mlp_body,
        out_shape=jax.ShapeDtypeStruct((seq_len, width), BF16),
        grid=(n_chunks,),
        in_specs=[whole, pl.BlockSpec((seq_len, q_width), lambda j: (0, 0)), whole,
                  rows_from(gate_at), rows_from(gate_at + ff_width), rows_from(q_width),
                  pl.BlockSpec((q_width, width), lambda j: (0, 0))],
        out_specs=whole,
        scratch_shapes=[pltpu.VMEM((seq_len, width), F32)],
        compiler_params=pltpu.CompilerParams(vmem_limit_bytes=60 * 1024 * 1024),
        name="mlp",
    )(h, attn, x, w_in_t, w_in_t, w_out, w_out)


def solution(mesh):
    tok_spec = P(('part', 'dp', 'tp'))

    def per_device(x_blk, ln_gain, w_in_blk, w_out_blk):
        _, seq_len, width = x_blk.shape
        x = x_blk[0]
        w_in_t = lax.all_gather(w_in_blk.T, ('dp', 'tp'), axis=0, tiled=True)
        w_out = lax.all_gather(w_out_blk, ('dp', 'tp'), axis=0, tiled=True)
        ff_width = 4 * width
        q_width = w_out.shape[0] - ff_width
        head_dim = (w_in_t.shape[0] - w_out.shape[0] - ff_width) // 2
        gate_at = q_width + 2 * head_dim
        cos_t, sin_t = rope_tables(seq_len, head_dim)
        h, attn, kt, vt = attention_call(x, ln_gain.reshape(1, width), w_in_t[:gate_at], jnp.asarray(cos_t),
                                         jnp.asarray(sin_t), q_width // head_dim, head_dim)
        y = mlp_call(h, attn, x, w_in_t, w_out, gate_at, ff_width)
        return y[None], kt.T[None], vt.T[None]

    return jax.shard_map(per_device, mesh=mesh,
                         in_specs=(tok_spec, P(), P(None, ('dp', 'tp')), P(('dp', 'tp'), None)),
                         out_specs=(tok_spec, tok_spec, tok_spec), check_vma=False)
```

time: 463 us -> 271 us (0.59)
  matrix products: 225 us -> 0 us
  Pallas kernels: 0 us -> 91.6 us
  other arithmetic: 35.6 us -> 0 us
  local copies, waits for them, and re-layouts: 45.2 us -> 27.5 us
  loops' own time: 10.4 us -> 0 us
  waiting for transfers between devices: 131 us -> 137 us
    dot_general x6 -> x0, matrix products: 127 us -> none  [the longest x4 76.7 us: one_block(): jnp.einsum('bqhk,bke->bqhe', attn_prob, v_all, preferred_element_type=jnp...]
    sub x4 -> x0, matrix products: 97.6 us -> none  [one_block(): attn_prob = jax.nn.softmax(scores, axis=-1).astype(jnp.bfloat16)]
    pallas_call x0 -> x2, Pallas kernels: none -> 91.6 us  [the longest x1 49.8 us: attention_call(): pl.pallas_call(functools.partial(attention_body, heads, head_dim), out_sh...]
    convert_element_type x2 -> x0, other arithmetic: 17.7 us -> none  [the longest x1 16.9 us: mix_rows(): (jax.nn.silu(gate_proj.astype(jnp.float32)) * up_proj.astype(jnp.float32)...]
    another operation x1 -> x0, loops' own time: 10.4 us -> none  [causal_mqa(): out_tiles = lax.map(one_block, jnp.arange(n_blk))]
    while x1 -> x0, local copies, waits for them, and re-layouts: 6.17 us -> none  [causal_mqa(): out_tiles = lax.map(one_block, jnp.arange(n_blk))]
    another operation x1 -> x0, local copies, waits for them, and re-layouts: 6.1 us -> none  [causal_mqa(): jnp.moveaxis(out_tiles, 0, 1).reshape(n_batch, seq_len, n_heads * head_dim)]
    all_gather x1, waiting for transfers between devices: 67.2 us -> 73 us  [per_device(): w_out = lax.all_gather(w_out_blk, ('dp', 'tp'), axis=0, tiled=True)]
where the time goes in v1:
time: 271 us; the launch traced here: 270 us
  waiting for transfers between devices  137 us (51%)
  Pallas kernels  91.6 us (34%)
  local copies, waits for them, and re-layouts  27.5 us (10%)
  between operations  14 us (5%)
    all_gather x1, waiting for transfers between devices, per_device(): w_out = lax.all_gather(w_out_blk, ('dp', 'tp'), axis=0, tiled=True)  73 us
    all_gather x1, waiting for transfers between devices, per_device(): w_in_t = lax.all_gather(w_in_blk.T, ('dp', 'tp'), axis=0, tiled=True)  62.4 us
    pallas_call x1, Pallas kernels, attention_call(): pl.pallas_call(functools.partial(attention_body, heads, head_dim), out_sh...  49.8 us
    pallas_call x1, Pallas kernels, mlp_call(): pl.pallas_call(mlp_body, out_shape=jax.ShapeDtypeStruct((seq_len, width),...  41.8 us
    unnamed x2, local copies, waits for them, and re-layouts  23.7 us
  transfers between devices with their start and end apart: 2, of which 2 were waited for; matrix products, arithmetic and copies ran while one was open for 4% of the time, Pallas kernels for 0%

profile of v1, /device:TPU:1, one launch (start us, length us, event | category | flops | bytes accessed | tf_op | source)
XLA Modules:
  0.0 270.0 jit_solution(1848314554990427667)
XLA Ops:
  7.2 0.0 all-gather.7.cloned.1.call-start
  7.2 0.7 all-gather.7.cloned.1.call-update
  7.9 0.0 all-gather.5.cloned.1.call-start
  7.9 0.7 all-gather.5.cloned.1.call-update
  8.6 1.3 reshape.9.gain_ref
  9.9 73.0 %all-gather.7.cloned.1.call-done = bf16[128,30,768]{2,1,0:T(8,128)(2,1)} async-done(((bf16[1,30,768]{2,1,0:T(8,128)(2,1)}), bf16[128,30,768]{2,1,0:T(8,128)(2,1)}) %all-gather.7.cloned.1.call-update) | async-done | bytes 5898256 | tf_op jit(solution)/shard_map/all_gather | solution.py:199
  83.0 9.4 %reshape.13.wd_ref.wa_ref = bf16[3840,768]{1,0:T(8,128)(2,1)} reshape(bf16[128,30,768]{2,1,0:T(8,128)(2,1)} %all-gather.7.cloned.1.call-done) | data formatting | bytes 11796480
  92.4 62.4 %all-gather.5.cloned.1.call-done = bf16[128,55,768]{2,1,0:T(8,128)(2,1)} async-done(((bf16[1,55,768]{2,1,0:T(8,128)(2,1)}), bf16[128,55,768]{2,1,0:T(8,128)(2,1)}) %all-gather.5.cloned.1.call-update) | async-done | bytes 10813456 | tf_op jit(solution)/shard_map/all_gather | solution.py:198
  154.8 14.3 %reshape.11.wg_ref.wu_ref = bf16[7040,768]{1,0:T(8,128)(2,1)} reshape(bf16[128,55,768]{2,1,0:T(8,128)(2,1)} %all-gather.5.cloned.1.call-done) | data formatting | bytes 21626880
  169.1 2.5 slice.4.wq_ref
  171.6 49.8 %attention.1 = (bf16[2048,768]{1,0:T(8,128)(2,1)}, bf16[2048,768]{1,0:T(8,128)(2,1)}, bf16[64,2048]{1,0:T(8,128)(2,1)}, bf16[64,2048]{1,0:T(8,128)(2,1)}) custom-call(bf16[2048,768]{1,0:T(8,128)(2,1)} %bitcast.12, f32[1,768]{1,0:T(1,128)} %reshape.9.gain_ref, bf16[896,768]{1,0:T(8,128)(2,1)} %slice.4.wq_ref, f32[32,2048]{1,0:T(8,128)} %constant.4.clone.cos_ref, ...), custom_call_target="tpu_custom_call" | custom-call | tf_op jit(solution)/shard_map/attention/pallas_call | solution.py:123
  221.4 41.8 %mlp.1 = bf16[2048,768]{1,0:T(8,128)(2,1)} custom-call(bf16[2048,768]{1,0:T(8,128)(2,1)} %get-tuple-element.7.h_ref, bf16[2048,768]{1,0:T(8,128)(2,1)} %get-tuple-element.8.attn_ref, bf16[2048,768]{1,0:T(8,128)(2,1)} %bitcast.13, bf16[7040,768]{1,0:T(8,128)(2,1)} %reshape.11.wg_ref.wu_ref, bf16[7040,768]{1,0:T(8,128)(2,1)} %reshape.11.wg_ref.wu_ref, ...), custom_call_target="tpu_custom_call" | custom-call | tf_op jit(solution)/shard_map/mlp/pallas_call | solution.py:178
Async XLA Ops:
  7.2 75.8 %all-gather.7.cloned.1.call-start = ((), (), s32[]{:S(2)}) async-start(), calls=%async_computation.1 | async-start | bytes 6340608 | tf_op jit(solution)/shard_map/all_gather | solution.py:199
  7.9 146.9 %all-gather.5.cloned.1.call-start = ((), (), s32[]{:S(2)}) async-start(), calls=%async_computation | async-start | bytes 11096064 | tf_op jit(solution)/shard_map/all_gather | solution.py:198
Sparse Core Ops, SparseCore 0:
  11.1 71.8 all-gather.6
  86.0 68.7 all-gather.4
